TPU v7x, 32 devices: a whole 2x2x4 slice. The times are simulated.
32 devices in a mesh: gx: 4 (over y, x), gy: 2 (over core), gz: 4 (over z).
Axes of the slice: x: 2, y: 2, z: 4, core: 2. Of those that a mesh axis runs over, the one named last changes fastest.
Arguments:
- gradient: float32 [4, 2, 4, 16, 512], P('gx', 'gy', 'gz'), may hold values from -60 to 60
- local_schur: bfloat16 [4, 2, 4, 2048, 2048], P('gx', 'gy', 'gz'), may hold values from -1 to 4
- inverse_rows: bfloat16 [4, 2, 4, 512, 2048], P('gx', 'gy', 'gz'), may hold values from -0.1 to 0.6
- face_maps: int32 [4, 2, 4, 6, 256], P('gx', 'gy', 'gz'), may hold values from 0 to 511, as said below
Outputs:
- adjoint: float32 [4, 2, 4, 16, 512], P('gx', 'gy', 'gz')
- residual_ratio: float32 [16], replicated
Inputs may be any that keep to these rules, and one draw needn't show every extreme that they name: `face_maps`: for each subdomain and face, 256 distinct owned rows of the neighbour across that face.
All inputs are finite; a program needn't handle non-finite values.
Results may differ from a plain program's by a relative error of at most 0.0038.
Values may be sent and summed in bfloat16 or wider, within the bound.
A program may use at most 64 MiB of HBM per device.

v0:
```python
import functools

import jax
import jax.numpy as jnp
from jax import lax
from jax.experimental import pallas as pl
from jax.experimental.pallas import tpu as pltpu
from jax.sharding import PartitionSpec as P

ITERS = 3
EPSILON = 1e-06
FAR = (0, 1)
NEAR = (4, 5, 2, 3)
MESH = pl.DeviceIdType.MESH
BF16 = jnp.bfloat16
F32 = jnp.float32


def split(x):
    high = x.astype(BF16)
    low = (x - high.astype(F32)).astype(BF16)
    return jnp.concatenate([high, low], axis=0)


def merge(x):
    rows = x.shape[0] // 2
    return x[:rows] + x[rows:]


def mm(a, b):
    return jnp.dot(a, b, preferred_element_type=F32)


def rotate_solve(columns, beta_norm):
    num_cols = len(columns)
    rhs_vec = [beta_norm] + [jnp.zeros_like(beta_norm) for unused in range(num_cols)]
    cosines = []
    sines = []
    triangle = []
    for section in range(num_cols):
        column = [columns[section][row_at] for row_at in range(section + 2)]
        for earlier in range(section):
            rotated_a = cosines[earlier] * column[earlier] + sines[earlier] * column[earlier + 1]
            rotated_b = -sines[earlier] * column[earlier] + cosines[earlier] * column[earlier + 1]
            column[earlier] = rotated_a
            column[earlier + 1] = rotated_b
        radius = jnp.sqrt(
            column[section] * column[section] + column[section + 1] * column[section + 1]
        )
        cosine = column[section] / radius
        sine_val = column[section + 1] / radius
        column[section] = radius
        cosines.append(cosine)
        sines.append(sine_val)
        rhs_vec[section + 1] = -sine_val * rhs_vec[section]
        rhs_vec[section] = cosine * rhs_vec[section]
        triangle.append(column[: section + 1])
    coeffs = [None] * num_cols
    for section in reversed(range(num_cols)):
        running = rhs_vec[section]
        for onward in range(section + 1, num_cols):
            running = running - triangle[onward][section] * coeffs[onward]
        coeffs[section] = running / triangle[section][section]
    return (coeffs, jnp.abs(rhs_vec[num_cols]))


def kernel(
    sizes, g_ref, maps_ref, k_hbm, b_hbm, out_ref, ratio_ref,
    k_ref, b_ref, near_maps, gather_ref, scatter_ref, send_buf, recv_buf, acc_ref,
    base_ref, t_ref, v_ref, z_ref, w_ref, last_ref, total_ref, plane_buf, line_buf,
    weight_sem, map_send, map_recv, send_sem, recv_sem,
    plane_send, plane_recv, line_send, line_recv,
):
    nx, ny, nz = sizes
    rhs, own = g_ref.shape
    face = maps_ref.shape[-1]
    ix, iy, iz = lax.axis_index("gx"), lax.axis_index("gy"), lax.axis_index("gz")
    spots = ((ix, nx), (ix, nx), (iy, ny), (iy, ny), (iz, nz), (iz, nz))
    exists = [
        spots[f][0] > 0 if f % 2 == 0 else spots[f][0] < spots[f][1] - 1 for f in range(6)
    ]

    def across(f):
        step = 2 * (f % 2) - 1
        place = [ix, iy, iz]
        place[f // 2] = place[f // 2] + step
        return tuple(place)

    faces = [f for f in FAR + NEAR if spots[f][1] > 1]
    far_width, near_width = len(FAR) * face, len(NEAR) * face
    far_columns = pl.ds(own, far_width)
    near_columns = pl.ds(own + far_width, near_width)
    plane = [
        (lax.rem(ix + dx, nx), lax.rem(iy + dy, ny))
        for dx in range(nx) for dy in range(ny) if dx or dy
    ]
    line = [lax.rem(iz + dz, nz) for dz in range(1, nz)]

    weights = [pltpu.make_async_copy(b_hbm, b_ref, weight_sem.at[0])]
    weights.append(
        pltpu.make_async_copy(k_hbm.at[pl.ds(0, own)], k_ref.at[pl.ds(0, own)], weight_sem.at[1])
    )
    ghosts = pl.ds(own, k_ref.shape[0] - own)
    weights.append(pltpu.make_async_copy(k_hbm.at[ghosts], k_ref.at[ghosts], weight_sem.at[2]))
    for copy in weights:
        copy.start()

    barrier = pltpu.get_barrier_semaphore()
    for px, py in plane:
        pl.semaphore_signal(barrier, inc=1, device_id=(px, py, iz), device_id_type=MESH)
    for pz in line:
        pl.semaphore_signal(barrier, inc=1, device_id=(ix, iy, pz), device_id_type=MESH)

    t_ref[...] = g_ref[...]
    v_ref[...] = jnp.zeros_like(v_ref)
    z_ref[...] = jnp.zeros_like(z_ref)
    w_ref[...] = jnp.zeros_like(w_ref)
    last_ref[...] = jnp.zeros_like(last_ref)
    total_ref[...] = jnp.zeros_like(total_ref)
    for f in range(6):
        @pl.when(jnp.logical_not(exists[f]))
        def _():
            near_maps[f] = jnp.full(near_maps.shape[1:], -1, jnp.int32)
            for e in range(3 * ITERS):
                recv_buf[e, f] = jnp.zeros(recv_buf.shape[2:], BF16)

    def map_copy(f, slot):
        return pltpu.make_async_remote_copy(
            src_ref=maps_ref, dst_ref=near_maps.at[slot], send_sem=map_send.at[f],
            recv_sem=map_recv.at[slot], device_id=across(f), device_id_type=MESH,
        )

    def face_copy(e, f, slot):
        return pltpu.make_async_remote_copy(
            src_ref=send_buf.at[e, f], dst_ref=recv_buf.at[e, slot], send_sem=send_sem.at[e, f],
            recv_sem=recv_sem.at[e, slot], device_id=across(f), device_id_type=MESH,
        )

    def plane_copy(r, peer, slot):
        mine = ix * ny + iy
        return pltpu.make_async_remote_copy(
            src_ref=plane_buf.at[r, mine], dst_ref=plane_buf.at[r, slot],
            send_sem=plane_send.at[r, peer[0] * ny + peer[1]], recv_sem=plane_recv.at[r, slot],
            device_id=(peer[0], peer[1], iz), device_id_type=MESH,
        )

    def line_copy(r, peer, slot):
        return pltpu.make_async_remote_copy(
            src_ref=line_buf.at[r, iz], dst_ref=line_buf.at[r, slot],
            send_sem=line_send.at[r, peer], recv_sem=line_recv.at[r, slot],
            device_id=(ix, iy, peer), device_id_type=MESH,
        )

    lanes = lax.broadcasted_iota(jnp.int32, (rhs, 128), 1)
    rows = lax.broadcasted_iota(jnp.int32, (rhs, 128), 0)
    group = 128 // rhs
    places = lax.rem(lanes, group)
    mine = lax.div(lanes, group) == rows

    def start_sums(r):
        t = t_ref[...]
        last = last_ref[...]
        packed = jnp.where(places == ITERS, jnp.sum(t * t, axis=1, keepdims=True), 0.0)
        for k in range(ITERS):
            v = v_ref[k]
            packed = jnp.where(places == k, jnp.sum(v * t, axis=1, keepdims=True), packed)
            packed = jnp.where(
                places == ITERS + 1 + k, jnp.sum(v * last, axis=1, keepdims=True), packed
            )
        packed = jnp.where(mine, packed, 0.0)
        plane_buf[r, ix * ny + iy] = jnp.sum(packed, axis=0, keepdims=True)
        for peer in plane:
            plane_copy(r, peer, ix * ny + iy).start()

    def pass_sums(r):
        for peer in plane:
            plane_copy(r, peer, peer[0] * ny + peer[1]).wait_recv()
        partial = plane_buf[r, 0]
        for at in range(1, nx * ny):
            partial = partial + plane_buf[r, at]
        line_buf[r, iz] = partial
        for peer in line:
            line_copy(r, peer, iz).start()

    def finish_sums(r):
        for peer in line:
            line_copy(r, peer, peer).wait_recv()
        total = line_buf[r, 0]
        for at in range(1, nz):
            total = total + line_buf[r, at]
        total_ref[r] = jnp.where(mine, total, 0.0)

    def pick(r, lane):
        return jnp.sum(jnp.where(places == lane, total_ref[r], 0.0), axis=1, keepdims=True)

    def heights(r, count):
        coeffs = [pick(r, k) for k in range(count)]
        running = pick(r, ITERS)
        for k in range(count):
            running = running - 2.0 * coeffs[k] * coeffs[k]
            for n in range(k + 1):
                element = coeffs[k] * pick(k + 1, ITERS + 1 + n) * coeffs[n]
                running = running + (element if n == k else 2.0 * element)
        return coeffs, jnp.sqrt(jnp.maximum(running, 0.0) + EPSILON)

    def arrived(e, group):
        for f in group:
            if f in faces:
                @pl.when(exists[f])
                def _():
                    face_copy(e, f, f).wait_recv()
        return jnp.concatenate([recv_buf[e, f] for f in sorted(group)], axis=1)

    def scattered(e, base):
        added = mm(arrived(e, NEAR), scatter_ref[pl.ds(far_width, near_width), :])
        added = added + mm(arrived(e, FAR), scatter_ref[pl.ds(0, far_width), :])
        return base + merge(added)

    def stage(e, group, pairs):
        for at, f in enumerate(sorted(group)):
            send_buf[e, f] = pairs[:, at * face : (at + 1) * face]

    def send(e, group):
        odd = lax.rem(ix, 2) == 1

        def start(f, when):
            if f in faces:
                @pl.when(jnp.logical_and(exists[f], when))
                def _():
                    face_copy(e, f, f ^ 1).start()

        if group is FAR:
            start(1, odd)
            start(0, True)
            start(1, jnp.logical_not(odd))
        else:
            for f in group:
                start(f, True)

    def precondition(e, ready):
        pair = split(t_ref[...])
        stage(e, FAR, split(merge(mm(pair, b_ref[:, far_columns]))))
        ready()
        send(e, FAR)
        stage(e, NEAR, split(merge(mm(pair, b_ref[:, near_columns]))))
        send(e, NEAR)
        base_ref[...] = merge(mm(pair, b_ref[:, pl.ds(0, own)]))

    def iteration(j, carry):
        first, second, third = 3 * j, 3 * j + 1, 3 * j + 2
        start_sums(j)

        @pl.when(j == 0)
        def _():
            for f in faces:
                @pl.when(exists[f])
                def _():
                    map_copy(f, f).wait_recv()
            for f in range(6):
                row = near_maps[f, f ^ 1]
                hot = lax.broadcasted_iota(jnp.int32, (own, face), 0) == row
                hot = jnp.where(hot, 1.0, 0.0)
                gather_ref[:, pl.ds(f * face, face)] = hot.astype(BF16)
                scatter_ref[pl.ds(f * face, face), :] = jnp.transpose(hot).astype(BF16)

        prepared = scattered(first, base_ref[...])
        pair = split(prepared)
        stage(second, FAR, mm(pair, gather_ref[:, pl.ds(0, far_width)]).astype(BF16))
        send(second, FAR)
        stage(second, NEAR, mm(pair, gather_ref[:, pl.ds(far_width, near_width)]).astype(BF16))
        send(second, NEAR)
        pass_sums(j)

        @pl.when(j == 0)
        def _():
            weights[1].wait()

        acc_ref[...] = mm(pair, k_ref[pl.ds(0, own), :])

        @pl.when(j == 0)
        def _():
            weights[2].wait()

        acc_ref[...] += mm(arrived(second, NEAR), k_ref[near_columns, :])
        left = arrived(second, FAR)

        def products(columns):
            return merge(acc_ref[:, columns] + mm(left, k_ref[far_columns, columns]))

        stage(third, FAR, split(products(far_columns)))
        send(third, FAR)
        stage(third, NEAR, split(products(near_columns)))
        send(third, NEAR)
        base = products(pl.ds(0, own))
        finish_sums(j)
        coeffs, height = heights(j, ITERS - 1)
        inverse = 1.0 / height
        newest = t_ref[...]
        for k in range(ITERS - 1):
            prepared = prepared - coeffs[k] * z_ref[k]
            newest = newest - coeffs[k] * v_ref[k]
        z_ref[j] = prepared * inverse
        newest = newest * inverse
        v_ref[j] = newest
        last_ref[...] = newest
        applied = scattered(third, base)
        for k in range(ITERS - 1):
            applied = applied - coeffs[k] * w_ref[k]
        applied = applied * inverse
        w_ref[j] = applied
        t_ref[...] = applied

        @pl.when(j < ITERS - 1)
        def _():
            precondition(3 * j + 3, lambda: None)

        return carry


    def ready():
        pl.semaphore_wait(barrier, len(plane) + len(line))

    weights[0].wait()
    precondition(0, ready)
    for f in faces:
        @pl.when(exists[f])
        def _():
            map_copy(f, f ^ 1).start()
    lax.fori_loop(0, ITERS, iteration, 0)
    start_sums(ITERS)
    pass_sums(ITERS)
    finish_sums(ITERS)
    beta_norm = heights(0, 0)[1]
    columns = []
    for section in range(ITERS):
        coeffs, height = heights(section + 1, section + 1)
        columns.append(coeffs + [height])
    solved, remainder = rotate_solve(columns, beta_norm)
    adjoint = solved[0] * z_ref[0]
    for k in range(1, ITERS):
        adjoint = adjoint + solved[k] * z_ref[k]
    out_ref[...] = adjoint
    spread = jnp.where(rows == lanes, remainder / beta_norm, 0.0)
    ratio_ref[...] = jnp.sum(spread, axis=0, keepdims=True)[:, :rhs]

    for f in faces:
        @pl.when(exists[f])
        def _():
            map_copy(f, f ^ 1).wait_send()
            for e in range(3 * ITERS):
                face_copy(e, f, f ^ 1).wait_send()
    for r in range(ITERS + 1):
        for peer in plane:
            plane_copy(r, peer, ix * ny + iy).wait_send()
        for peer in line:
            line_copy(r, peer, iz).wait_send()


def local(sizes, gradient, local_schur, inverse_rows, face_maps):
    nx, ny, nz = sizes
    target = gradient[0, 0, 0]
    rhs, own = target.shape
    maps = jnp.swapaxes(face_maps[0, 0], 0, 1)
    face = maps.shape[-1]
    whole = local_schur.shape[-1]
    exchanges = 3 * ITERS
    sums = ITERS + 1
    vmem = pl.BlockSpec(memory_space=pltpu.VMEM)
    hbm = pl.BlockSpec(memory_space=pl.ANY)
    dma = pltpu.SemaphoreType.DMA
    adjoint, ratio = pl.pallas_call(
        functools.partial(kernel, sizes),
        out_shape=(
            pltpu.VMEM((rhs, own), F32),
            pltpu.VMEM((1, rhs), F32),
        ),
        in_specs=[vmem, vmem, hbm, hbm],
        out_specs=(vmem, vmem),
        scratch_shapes=[
            pltpu.VMEM((whole, whole), BF16),
            pltpu.VMEM((own, whole), BF16),
            pltpu.VMEM((6,) + maps.shape, jnp.int32),
            pltpu.VMEM((own, 6 * face), BF16),
            pltpu.VMEM((6 * face, own), BF16),
            pltpu.VMEM((exchanges, 6, 2 * rhs, face), BF16),
            pltpu.VMEM((exchanges, 6, 2 * rhs, face), BF16),
            pltpu.VMEM((2 * rhs, whole), F32),
            pltpu.VMEM((rhs, own), F32),
            pltpu.VMEM((rhs, own), F32),
            pltpu.VMEM((ITERS, rhs, own), F32),
            pltpu.VMEM((ITERS, rhs, own), F32),
            pltpu.VMEM((ITERS, rhs, own), F32),
            pltpu.VMEM((rhs, own), F32),
            pltpu.VMEM((sums, rhs, 128), F32),
            pltpu.VMEM((sums, nx * ny, 1, 128), F32),
            pltpu.VMEM((sums, nz, 1, 128), F32),
            dma((3,)),
            dma((6,)),
            dma((6,)),
            dma((exchanges, 6)),
            dma((exchanges, 6)),
            dma((sums, nx * ny)),
            dma((sums, nx * ny)),
            dma((sums, nz)),
            dma((sums, nz)),
        ],
        compiler_params=pltpu.CompilerParams(
            collective_id=0, has_side_effects=True, vmem_limit_bytes=56 * 1024 * 1024
        ),
    )(target, maps, local_schur[0, 0, 0], inverse_rows[0, 0, 0])
    return (adjoint[None, None, None], ratio[0])


def solution(mesh):
    placed = P("gx", "gy", "gz", None, None)
    sizes = (mesh.shape["gx"], mesh.shape["gy"], mesh.shape["gz"])
    return jax.shard_map(
        functools.partial(local, sizes),
        mesh=mesh,
        in_specs=(placed, placed, placed, placed),
        out_specs=(placed, P()),
        check_vma=False,
    )
```

profile of v0, /device:TPU:0, one launch (start us, length us, event | category | flops | bytes accessed | tf_op | source)
XLA Modules:
  0.0 51.6 jit_solution(115103890857314983)
XLA Ops:
  0.6 49.8 %shard_map.59 = (f32[16,512]{1,0:T(8,128)S(1)}, f32[1,16]{1,0:T(1,128)S(1)}) custom-call(f32[16,512]{1,0:T(8,128)} %bitcast.10, s32[6,1,256]{2,1,0:T(1,128)} %bitcast.11, bf16[2048,2048]{1,0:T(8,128)(2,1)} %bitcast.8, bf16[512,2048]{1,0:T(8,128)(2,1)} %bitcast.9), custom_call_target="tpu_custom_call" | custom-call | tf_op jit(solution)/shard_map/pallas_call | solution.py:371
  50.5 0.6 %copy.8 = f32[1,1,1,16,512]{4,3,2,1,0:T(8,128)} copy(f32[1,1,1,16,512]{4,3,2,1,0:T(8,128)S(1)} %bitcast.6) | data formatting | bytes 65536
  51.1 0.5 copy.9
where the time goes:
time: 51.8 us; the launch traced here: 51.6 us
  Pallas kernels  49.8 us (96%)
  local copies, waits for them, and re-layouts  1.13 us (2%)
  between operations  0.64 us (1%)
    pallas_call x1, Pallas kernels, local(): pl.pallas_call(functools.partial(kernel, sizes), out_shape=(pltpu.VMEM((r...  49.8 us
    unnamed x2, local copies, waits for them, and re-layouts  1.13 us

commit v1 on v0

v1 whole, which is shorter than its diff:
```python
import functools

import jax
import jax.numpy as jnp
from jax import lax
from jax.experimental import pallas as pl
from jax.experimental.pallas import tpu as pltpu
from jax.sharding import PartitionSpec as P

ITERS = 3
EPSILON = 1e-06
MESH = pl.DeviceIdType.MESH
BF16 = jnp.bfloat16
F32 = jnp.float32
DIRECT_MAX = 32


def split(x):
    high = x.astype(BF16)
    low = (x - high.astype(F32)).astype(BF16)
    return jnp.concatenate([high, low], axis=0)


def merge(x):
    rows = x.shape[0] // 2
    return x[:rows] + x[rows:]


def mm(a, b):
    return jnp.dot(a, b, preferred_element_type=F32)


def rotate_column(column, section, cosines, sines, rhs_vec, triangle):
    column = list(column)
    for earlier in range(section):
        rotated_a = cosines[earlier] * column[earlier] + sines[earlier] * column[earlier + 1]
        rotated_b = -sines[earlier] * column[earlier] + cosines[earlier] * column[earlier + 1]
        column[earlier] = rotated_a
        column[earlier + 1] = rotated_b
    radius = jnp.sqrt(
        column[section] * column[section] + column[section + 1] * column[section + 1]
    )
    cosine = column[section] / radius
    sine_val = column[section + 1] / radius
    column[section] = radius
    cosines.append(cosine)
    sines.append(sine_val)
    rhs_vec[section + 1] = -sine_val * rhs_vec[section]
    rhs_vec[section] = cosine * rhs_vec[section]
    triangle.append(column[: section + 1])


def back_substitute(rhs_vec, triangle):
    num_cols = len(triangle)
    coeffs = [None] * num_cols
    for section in reversed(range(num_cols)):
        running = rhs_vec[section]
        for onward in range(section + 1, num_cols):
            running = running - triangle[onward][section] * coeffs[onward]
        coeffs[section] = running / triangle[section][section]
    return coeffs


class Axis:
    def __init__(self, axis, spot, size, own, face, at):
        self.axis = axis
        self.single = size == 2
        low, high = spot > 0, spot < size - 1
        if self.single:
            which = 2 * axis + jnp.where(low, 0, 1)
            self.faces = [(2 * axis, 2 * axis, which, None, jnp.where(low, -1, 1))]
            self.width = face
            self.start = pl.multiple_of(own + which * face, face)
        else:
            self.faces = [
                (2 * axis, 2 * axis + 1, 2 * axis, low, -1),
                (2 * axis + 1, 2 * axis, 2 * axis + 1, high, 1),
            ]
            self.width = 2 * face
            self.start = own + 2 * axis * face
        self.columns = pl.ds(self.start, self.width)
        self.packed = pl.ds(at, self.width)


def kernel(
    sizes, g_ref, maps_ref, k_hbm, b_hbm, out_ref,
    k_ref, b_ref, near_maps, gather_ref, scatter_ref, send_buf, recv_buf, acc_ref,
    base_ref, t_ref, v_ref, z_ref, w_ref, last_ref, total_ref, plane_buf, line_buf, all_buf,
    weight_sem, map_send, map_recv, send_sem, recv_sem,
    plane_send, plane_recv, line_send, line_recv, all_send, all_recv,
):
    nx, ny, nz = sizes
    count = nx * ny * nz
    direct = count <= DIRECT_MAX
    rhs, own = g_ref.shape
    face = maps_ref.shape[-1]
    whole = k_ref.shape[0]
    ix, iy, iz = lax.axis_index("gx"), lax.axis_index("gy"), lax.axis_index("gz")
    here = (ix, iy, iz)

    groups = []
    at = 0
    for axis in range(3):
        if sizes[axis] > 1:
            groups.append(Axis(axis, here[axis], sizes[axis], own, face, at))
            at += groups[-1].width
    sending = [group for axis in (0, 2, 1) for group in groups if group.axis == axis]
    arriving = [group for axis in (1, 2, 0) for group in groups if group.axis == axis]
    final = arriving[-1]
    own_columns = pl.ds(0, own)

    def across(axis, step):
        place = list(here)
        place[axis] = place[axis] + step
        return tuple(place)

    def guarded(exists, body):
        if exists is None:
            body()
        else:
            pl.when(exists)(body)

    plane = [
        (lax.rem(ix + dx, nx), lax.rem(iy + dy, ny))
        for dx in range(nx) for dy in range(ny) if dx or dy
    ]
    line = [lax.rem(iz + dz, nz) for dz in range(1, nz)]
    others = [
        (lax.rem(ix + dx, nx), lax.rem(iy + dy, ny), lax.rem(iz + dz, nz))
        for dx in range(nx) for dy in range(ny) for dz in range(nz) if dx or dy or dz
    ]

    load_b = pltpu.make_async_copy(b_hbm, b_ref, weight_sem.at[0])
    load_own = pltpu.make_async_copy(
        k_hbm.at[pl.ds(0, own)], k_ref.at[pl.ds(0, own)], weight_sem.at[1]
    )
    ghosts = pl.ds(own, whole - own)
    load_ghosts = pltpu.make_async_copy(k_hbm.at[ghosts], k_ref.at[ghosts], weight_sem.at[2])
    load_b.start()

    barrier = pltpu.get_barrier_semaphore()
    greeted = [(px, py, iz) for px, py in plane] + [(ix, iy, pz) for pz in line]
    for peer in greeted:
        pl.semaphore_signal(barrier, inc=1, device_id=peer, device_id_type=MESH)

    t_ref[...] = g_ref[...]
    v_ref[...] = jnp.zeros_like(v_ref)
    z_ref[...] = jnp.zeros_like(z_ref)
    w_ref[...] = jnp.zeros_like(w_ref)
    last_ref[...] = jnp.zeros_like(last_ref)
    total_ref[...] = jnp.zeros_like(total_ref)
    for group in groups:
        for slot, _, _, exists, _ in group.faces:
            if exists is not None:
                @pl.when(jnp.logical_not(exists))
                def _():
                    near_maps[slot] = jnp.full(near_maps.shape[1:], -1, jnp.int32)
                    for e in range(3 * ITERS):
                        recv_buf[e, slot] = jnp.zeros(recv_buf.shape[2:], BF16)

    def map_copy(group, entry):
        slot, target, which, _, step = entry
        return pltpu.make_async_remote_copy(
            src_ref=maps_ref.at[which], dst_ref=near_maps.at[target],
            send_sem=map_send.at[slot], recv_sem=map_recv.at[target],
            device_id=across(group.axis, step), device_id_type=MESH,
        )

    def map_wait(group, entry):
        slot, _, which, _, step = entry
        return pltpu.make_async_remote_copy(
            src_ref=maps_ref.at[which], dst_ref=near_maps.at[slot],
            send_sem=map_send.at[slot], recv_sem=map_recv.at[slot],
            device_id=across(group.axis, step), device_id_type=MESH,
        )

    def face_copy(e, group, entry, arrival=False):
        slot, target, _, _, step = entry
        into = slot if arrival else target
        return pltpu.make_async_remote_copy(
            src_ref=send_buf.at[e, slot], dst_ref=recv_buf.at[e, into],
            send_sem=send_sem.at[e, slot], recv_sem=recv_sem.at[e, into],
            device_id=across(group.axis, step), device_id_type=MESH,
        )

    def plane_copy(r, peer, slot):
        mine = ix * ny + iy
        return pltpu.make_async_remote_copy(
            src_ref=plane_buf.at[r, mine], dst_ref=plane_buf.at[r, slot],
            send_sem=plane_send.at[r, peer[0] * ny + peer[1]], recv_sem=plane_recv.at[r, slot],
            device_id=(peer[0], peer[1], iz), device_id_type=MESH,
        )

    def line_copy(r, peer, slot):
        return pltpu.make_async_remote_copy(
            src_ref=line_buf.at[r, iz], dst_ref=line_buf.at[r, slot],
            send_sem=line_send.at[r, peer], recv_sem=line_recv.at[r, slot],
            device_id=(ix, iy, peer), device_id_type=MESH,
        )

    def rank(peer):
        return (peer[0] * ny + peer[1]) * nz + peer[2]

    def all_copy(peer, slot):
        return pltpu.make_async_remote_copy(
            src_ref=all_buf.at[rank(here)], dst_ref=all_buf.at[slot],
            send_sem=all_send.at[rank(peer)], recv_sem=all_recv.at[slot],
            device_id=peer, device_id_type=MESH,
        )

    lanes = lax.broadcasted_iota(jnp.int32, (rhs, 128), 1)
    rows = lax.broadcasted_iota(jnp.int32, (rhs, 128), 0)
    spread = 128 // rhs
    places = lax.rem(lanes, spread)
    mine = lax.div(lanes, spread) == rows

    def packed_sums():
        t = t_ref[...]
        last = last_ref[...]
        packed = jnp.where(places == ITERS, jnp.sum(t * t, axis=1, keepdims=True), 0.0)
        for k in range(ITERS):
            v = v_ref[k]
            packed = jnp.where(places == k, jnp.sum(v * t, axis=1, keepdims=True), packed)
            packed = jnp.where(
                places == ITERS + 1 + k, jnp.sum(v * last, axis=1, keepdims=True), packed
            )
        return jnp.sum(jnp.where(mine, packed, 0.0), axis=0, keepdims=True)

    def start_sums(r):
        plane_buf[r, ix * ny + iy] = packed_sums()
        for peer in plane:
            plane_copy(r, peer, ix * ny + iy).start()

    def pass_sums(r):
        for peer in plane:
            plane_copy(r, peer, peer[0] * ny + peer[1]).wait_recv()
        partial = plane_buf[r, 0]
        for at in range(1, nx * ny):
            partial = partial + plane_buf[r, at]
        line_buf[r, iz] = partial
        for peer in line:
            line_copy(r, peer, iz).start()

    def finish_sums(r):
        for peer in line:
            line_copy(r, peer, peer).wait_recv()
        total = line_buf[r, 0]
        for at in range(1, nz):
            total = total + line_buf[r, at]
        total_ref[r] = jnp.where(mine, total, 0.0)

    def pick(r, lane):
        return jnp.sum(jnp.where(places == lane, total_ref[r], 0.0), axis=1, keepdims=True)

    def heights(r, count):
        coeffs = [pick(r, k) for k in range(count)]
        running = pick(r, ITERS)
        for k in range(count):
            running = running - 2.0 * coeffs[k] * coeffs[k]
            for n in range(k + 1):
                element = coeffs[k] * pick(k + 1, ITERS + 1 + n) * coeffs[n]
                running = running + (element if n == k else 2.0 * element)
        return coeffs, jnp.sqrt(jnp.maximum(running, 0.0) + EPSILON)

    def arrived(e, group):
        for entry in group.faces:
            guarded(entry[3], lambda: face_copy(e, group, entry, True).wait_recv())
        blocks = [recv_buf[e, entry[0]] for entry in group.faces]
        return blocks[0] if len(blocks) == 1 else jnp.concatenate(blocks, axis=1)

    def scattered(e, base):
        for group in arriving:
            base = base + mm(arrived(e, group), scatter_ref[group.packed, :])
        return base

    def send(e, group, values):
        values = values.astype(BF16)
        for at, entry in enumerate(group.faces):
            send_buf[e, entry[0]] = values[:, at * face : (at + 1) * face]

        def start(entry, when=None):
            exists = entry[3]
            if when is not None:
                exists = when if exists is None else jnp.logical_and(exists, when)
            guarded(exists, lambda: face_copy(e, group, entry).start())

        if group is final and len(group.faces) == 2:
            odd = lax.rem(here[group.axis], 2) == 1
            start(group.faces[1], odd)
            start(group.faces[0])
            start(group.faces[1], jnp.logical_not(odd))
        else:
            for entry in group.faces:
                start(entry)

    def precondition(e, ready):
        pair = split(t_ref[...])
        first = True
        for group in sending:
            values = merge(mm(pair, b_ref[:, group.columns]))
            if first:
                ready()
                first = False
            send(e, group, values)
        base_ref[...] = merge(mm(pair, b_ref[:, own_columns]))

    def iteration(j, carry):
        first, second, third = 3 * j, 3 * j + 1, 3 * j + 2
        start_sums(j)

        @pl.when(j == 0)
        def _():
            for group in groups:
                for at, entry in enumerate(group.faces):
                    guarded(entry[3], lambda: map_wait(group, entry).wait_recv())
                    row = near_maps[entry[0]]
                    hot = lax.broadcasted_iota(jnp.int32, (own, face), 0) == row
                    hot = jnp.where(hot, 1.0, 0.0)
                    part = pl.ds(group.packed.start + at * face, face)
                    gather_ref[:, part] = hot.astype(BF16)
                    scatter_ref[part, :] = jnp.transpose(hot).astype(BF16)

        prepared = scattered(first, base_ref[...])
        rounded = prepared.astype(BF16)
        for group in sending:
            send(second, group, mm(rounded, gather_ref[:, group.packed]))
        pair = split(prepared)
        pass_sums(j)

        @pl.when(j == 0)
        def _():
            load_own.wait()

        targets = [group.columns for group in sending] + [own_columns]
        for columns in targets:
            acc_ref[:, columns] = merge(mm(pair, k_ref[own_columns, columns]))

        @pl.when(j == 0)
        def _():
            load_ghosts.wait()

        for group in arriving[:-1]:
            values = arrived(second, group)
            for columns in targets:
                acc_ref[:, columns] += mm(values, k_ref[group.columns, columns])
        values = arrived(second, final)

        def products(columns):
            return acc_ref[:, columns] + mm(values, k_ref[final.columns, columns])

        for group in sending:
            send(third, group, products(group.columns))
        base = products(own_columns)
        finish_sums(j)
        coeffs, height = heights(j, ITERS - 1)
        inverse = 1.0 / height
        newest = t_ref[...]
        for k in range(ITERS - 1):
            prepared = prepared - coeffs[k] * z_ref[k]
            newest = newest - coeffs[k] * v_ref[k]
        z_ref[j] = prepared * inverse
        newest = newest * inverse
        v_ref[j] = newest
        last_ref[...] = newest
        applied = scattered(third, base)
        for k in range(ITERS - 1):
            applied = applied - coeffs[k] * w_ref[k]
        applied = applied * inverse
        w_ref[j] = applied
        t_ref[...] = applied

        @pl.when(j < ITERS - 1)
        def _():
            precondition(3 * j + 3, lambda: None)

        return carry

    def ready():
        load_own.start()
        load_ghosts.start()
        pl.semaphore_wait(barrier, len(greeted))
        for group in groups:
            for entry in group.faces:
                guarded(entry[3], lambda: map_copy(group, entry).start())

    load_b.wait()
    precondition(0, ready)
    lax.fori_loop(0, ITERS, iteration, 0)
    if direct:
        all_buf[rank(here)] = packed_sums()
        for peer in others:
            all_copy(peer, rank(here)).start()
    else:
        start_sums(ITERS)
        pass_sums(ITERS)
    beta_norm = heights(0, 0)[1]
    rhs_vec = [beta_norm] + [jnp.zeros_like(beta_norm)] * ITERS
    cosines, sines, triangle = [], [], []
    for section in range(ITERS - 1):
        coeffs, height = heights(section + 1, section + 1)
        rotate_column(coeffs + [height], section, cosines, sines, rhs_vec, triangle)
    if direct:
        for peer in others:
            all_copy(peer, rank(peer)).wait_recv()
        total = jnp.sum(all_buf[...], axis=0)
        total_ref[ITERS] = jnp.where(mine, total, 0.0)
    else:
        finish_sums(ITERS)
    coeffs, height = heights(ITERS, ITERS)
    rotate_column(coeffs + [height], ITERS - 1, cosines, sines, rhs_vec, triangle)
    solved = back_substitute(rhs_vec, triangle)
    adjoint = solved[0] * z_ref[0]
    for k in range(1, ITERS):
        adjoint = adjoint + solved[k] * z_ref[k]
    out_ref[pl.ds(0, rhs), :] = adjoint
    ratio = jnp.abs(rhs_vec[ITERS]) / beta_norm
    ratio = jnp.sum(jnp.where(rows == lanes, ratio, 0.0), axis=0, keepdims=True)
    out_ref[pl.ds(rhs, 8), pl.ds(0, 128)] = jnp.broadcast_to(ratio, (8, 128))

    for group in groups:
        for entry in group.faces:
            def drain():
                map_copy(group, entry).wait_send()
                for e in range(3 * ITERS):
                    face_copy(e, group, entry).wait_send()
            guarded(entry[3], drain)
    for r in range(ITERS if direct else ITERS + 1):
        for peer in plane:
            plane_copy(r, peer, ix * ny + iy).wait_send()
        for peer in line:
            line_copy(r, peer, iz).wait_send()
    if direct:
        for peer in others:
            all_copy(peer, rank(here)).wait_send()


def local(sizes, gradient, local_schur, inverse_rows, face_maps):
    nx, ny, nz = sizes
    target = gradient[0, 0, 0]
    rhs, own = target.shape
    maps = jnp.swapaxes(face_maps[0, 0], 0, 1)
    face = maps.shape[-1]
    whole = local_schur.shape[-1]
    exchanges = 3 * ITERS
    sums = ITERS + 1
    count = nx * ny * nz
    direct = count if count <= DIRECT_MAX else 1
    vmem = pl.BlockSpec(memory_space=pltpu.VMEM)
    hbm = pl.BlockSpec(memory_space=pl.ANY)
    dma = pltpu.SemaphoreType.DMA
    packed = pl.pallas_call(
        functools.partial(kernel, sizes),
        out_shape=pltpu.VMEM((rhs + 8, own), F32),
        in_specs=[vmem, vmem, hbm, hbm],
        out_specs=vmem,
        scratch_shapes=[
            pltpu.VMEM((whole, whole), BF16),
            pltpu.VMEM((own, whole), BF16),
            pltpu.VMEM(maps.shape, jnp.int32),
            pltpu.VMEM((own, 6 * face), BF16),
            pltpu.VMEM((6 * face, own), BF16),
            pltpu.VMEM((exchanges, 6, rhs, face), BF16),
            pltpu.VMEM((exchanges, 6, rhs, face), BF16),
            pltpu.VMEM((rhs, whole), F32),
            pltpu.VMEM((rhs, own), F32),
            pltpu.VMEM((rhs, own), F32),
            pltpu.VMEM((ITERS, rhs, own), F32),
            pltpu.VMEM((ITERS, rhs, own), F32),
            pltpu.VMEM((ITERS, rhs, own), F32),
            pltpu.VMEM((rhs, own), F32),
            pltpu.VMEM((sums, rhs, 128), F32),
            pltpu.VMEM((sums, nx * ny, 1, 128), F32),
            pltpu.VMEM((sums, nz, 1, 128), F32),
            pltpu.VMEM((direct, 1, 128), F32),
            dma((3,)),
            dma((6,)),
            dma((6,)),
            dma((exchanges, 6)),
            dma((exchanges, 6)),
            dma((sums, nx * ny)),
            dma((sums, nx * ny)),
            dma((sums, nz)),
            dma((sums, nz)),
            dma((direct,)),
            dma((direct,)),
        ],
        compiler_params=pltpu.CompilerParams(
            collective_id=0, has_side_effects=True, vmem_limit_bytes=56 * 1024 * 1024
        ),
    )(target, maps, local_schur[0, 0, 0], inverse_rows[0, 0, 0])
    return (packed[None, None, None, :rhs], packed[rhs, :rhs])


def solution(mesh):
    placed = P("gx", "gy", "gz", None, None)
    sizes = (mesh.shape["gx"], mesh.shape["gy"], mesh.shape["gz"])
    return jax.shard_map(
        functools.partial(local, sizes),
        mesh=mesh,
        in_specs=(placed, placed, placed, placed),
        out_specs=(placed, P()),
        check_vma=False,
    )
```

time: 51.8 us -> 46.9 us (0.905)
  Pallas kernels: 49.8 us -> 45 us
    pallas_call x1, Pallas kernels: 49.8 us -> 45 us  [local(): pl.pallas_call(functools.partial(kernel, sizes), out_shape=pltpu.VMEM((rh...]
    unnamed x2 -> x0, local copies, waits for them, and re-layouts: 1.13 us -> none
    broadcast_in_dim x0 -> x1, local copies, waits for them, and re-layouts: none -> 0.62 us  [local(): return (packed[None, None, None, :rhs], packed[rhs, :rhs])]
where the time goes in v1:
time: 46.9 us; the launch traced here: 46.7 us
  Pallas kernels  45 us (96%)
  local copies, waits for them, and re-layouts  1.13 us (2%)
  between operations  0.64 us (1%)
    pallas_call x1, Pallas kernels, local(): pl.pallas_call(functools.partial(kernel, sizes), out_shape=pltpu.VMEM((rh...  45 us

profile of v1, /device:TPU:0, one launch (start us, length us, event | category | flops | bytes accessed | tf_op | source)
XLA Modules:
  0.0 46.7 jit_solution(5914960901533593375)
XLA Ops:
  0.6 45.0 %shard_map.59 = f32[24,512]{1,0:T(8,128)S(1)} custom-call(f32[16,512]{1,0:T(8,128)} %bitcast.10, s32[6,1,256]{2,1,0:T(1,128)} %bitcast.11, bf16[2048,2048]{1,0:T(8,128)(2,1)} %bitcast.8, bf16[512,2048]{1,0:T(8,128)(2,1)} %bitcast.9), custom_call_target="tpu_custom_call" | custom-call | tf_op jit(solution)/shard_map/pallas_call | solution.py:451
  45.6 0.5 %slice_bitcast_fusion.1 = f32[16]{0:T(128)} fusion(f32[24,512]{1,0:T(8,128)S(1)} %shard_map.59), kind=kLoop, calls=%fused_computation.1 | loop fusion | bytes 128 | tf_op jit(solution)/shard_map/squeeze | solution.py:491
  46.1 0.6 %slice_bitcast_fusion = f32[1,1,1,16,512]{4,3,2,1,0:T(8,128)} fusion(f32[24,512]{1,0:T(8,128)S(1)} %shard_map.59), kind=kLoop, calls=%fused_computation | loop fusion | bytes 65536 | tf_op jit(solution)/shard_map/broadcast_in_dim | solution.py:491

commit v2 on v1

--- a/solution.py
+++ b/solution.py
@@ -13,6 +13,7 @@
 BF16 = jnp.bfloat16
 F32 = jnp.float32
 DIRECT_MAX = 32
+PAIRED = (False, True, True)
 
 
 def split(x):
@@ -83,8 +84,8 @@
 
 
 def kernel(
-    sizes, g_ref, maps_ref, k_hbm, b_hbm, out_ref,
-    k_ref, b_ref, near_maps, gather_ref, scatter_ref, send_buf, recv_buf, acc_ref,
+    sizes, g_hbm, maps_hbm, k_hbm, b_hbm, out_ref,
+    g_ref, maps_ref, k_ref, b_ref, near_maps, cols_ref, inverse_ref, send_buf, recv_buf, acc_ref,
     base_ref, t_ref, v_ref, z_ref, w_ref, last_ref, total_ref, plane_buf, line_buf, all_buf,
     weight_sem, map_send, map_recv, send_sem, recv_sem,
     plane_send, plane_recv, line_send, line_recv, all_send, all_recv,
@@ -136,14 +137,29 @@
     )
     ghosts = pl.ds(own, whole - own)
     load_ghosts = pltpu.make_async_copy(k_hbm.at[ghosts], k_ref.at[ghosts], weight_sem.at[2])
+    load_g = pltpu.make_async_copy(g_hbm, g_ref, weight_sem.at[3])
+    load_maps = pltpu.make_async_copy(maps_hbm, maps_ref, weight_sem.at[4])
+    load_maps.start()
+    load_g.start()
     load_b.start()
 
     barrier = pltpu.get_barrier_semaphore()
-    greeted = [(px, py, iz) for px, py in plane] + [(ix, iy, pz) for pz in line]
-    for peer in greeted:
-        pl.semaphore_signal(barrier, inc=1, device_id=peer, device_id_type=MESH)
-
-    t_ref[...] = g_ref[...]
+    greeted = [((px, py, iz), None) for px, py in plane]
+    if nz <= 4:
+        greeted += [
+            (across(2, dz), iz + dz >= 0 if dz < 0 else iz + dz < nz)
+            for dz in (-2, -1, 1, 2) if abs(dz) < nz
+        ]
+    else:
+        greeted += [((ix, iy, pz), None) for pz in line]
+    expected = 0
+    for peer, exists in greeted:
+        expected = expected + (1 if exists is None else exists.astype(jnp.int32))
+        guarded(exists, lambda: pl.semaphore_signal(
+            barrier, inc=1, device_id=peer, device_id_type=MESH
+        ))
+
+    cols_ref[...] = jnp.full(cols_ref.shape, -1, jnp.int32)
     v_ref[...] = jnp.zeros_like(v_ref)
     z_ref[...] = jnp.zeros_like(z_ref)
     w_ref[...] = jnp.zeros_like(w_ref)
@@ -155,8 +171,9 @@
                 @pl.when(jnp.logical_not(exists))
                 def _():
                     near_maps[slot] = jnp.full(near_maps.shape[1:], -1, jnp.int32)
-                    for e in range(3 * ITERS):
-                        recv_buf[e, slot] = jnp.zeros(recv_buf.shape[2:], BF16)
+                    for stage in range(3):
+                        for j in range(ITERS):
+                            recv_buf[stage, j, slot] = jnp.zeros(recv_buf.shape[3:], BF16)
 
     def map_copy(group, entry):
         slot, target, which, _, step = entry
@@ -174,12 +191,16 @@
             device_id=across(group.axis, step), device_id_type=MESH,
         )
 
-    def face_copy(e, group, entry, arrival=False):
+    def height_of(stage):
+        return pl.ds(0, 2 * rhs if PAIRED[stage] else rhs)
+
+    def face_copy(stage, j, group, entry, arrival=False):
         slot, target, _, _, step = entry
         into = slot if arrival else target
         return pltpu.make_async_remote_copy(
-            src_ref=send_buf.at[e, slot], dst_ref=recv_buf.at[e, into],
-            send_sem=send_sem.at[e, slot], recv_sem=recv_sem.at[e, into],
+            src_ref=send_buf.at[stage, j, slot, height_of(stage)],
+            dst_ref=recv_buf.at[stage, j, into, height_of(stage)],
+            send_sem=send_sem.at[stage, j, slot], recv_sem=recv_sem.at[stage, j, into],
             device_id=across(group.axis, step), device_id_type=MESH,
         )
 
@@ -262,27 +283,67 @@
                 running = running + (element if n == k else 2.0 * element)
         return coeffs, jnp.sqrt(jnp.maximum(running, 0.0) + EPSILON)
 
-    def arrived(e, group):
+    def arrived(stage, j, group):
         for entry in group.faces:
-            guarded(entry[3], lambda: face_copy(e, group, entry, True).wait_recv())
-        blocks = [recv_buf[e, entry[0]] for entry in group.faces]
+            guarded(entry[3], lambda: face_copy(stage, j, group, entry, True).wait_recv())
+        blocks = [recv_buf[stage, j, entry[0], height_of(stage)] for entry in group.faces]
         return blocks[0] if len(blocks) == 1 else jnp.concatenate(blocks, axis=1)
 
-    def scattered(e, base):
+    def joined(stage, product):
+        return merge(product) if PAIRED[stage] else product
+
+    def rounded(stage, values):
+        return split(values) if PAIRED[stage] else values.astype(BF16)
+
+    def take(values, index):
+        sources = [values[:, at : at + 128] for at in range(0, values.shape[1], 128)]
+        taken = []
+        for at in range(0, index.shape[1], 128):
+            spots = jnp.broadcast_to(index[:, at : at + 128], (rhs, 128))
+            low = jnp.bitwise_and(spots, 127)
+            high = jnp.right_shift(spots, 7)
+            out = jnp.zeros((rhs, 128), F32)
+            for k, source in enumerate(sources):
+                picked = jnp.take_along_axis(source, low, axis=1, mode="promise_in_bounds")
+                out = jnp.where(high == k, picked, out)
+            taken.append(out)
+        return jnp.concatenate(taken, axis=1)
+
+    def scattered(stage, j, base):
         for group in arriving:
-            base = base + mm(arrived(e, group), scatter_ref[group.packed, :])
+            for entry in group.faces:
+                guarded(entry[3], lambda: face_copy(stage, j, group, entry, True).wait_recv())
+                block = recv_buf[stage, j, entry[0], height_of(stage)].astype(F32)
+                base = base + take(joined(stage, block), inverse_ref[entry[0]])
         return base
 
-    def send(e, group, values):
-        values = values.astype(BF16)
+    def found(column, targets):
+        order = lax.broadcasted_iota(jnp.int32, targets.shape, 0).astype(F32) + 1.0
+        matched = jnp.where(column == targets, order, 0.0)
+        return jnp.sum(matched, axis=0, keepdims=True).astype(jnp.int32) - 1
+
+    def invert():
+        for group in groups:
+            for entry in group.faces:
+                guarded(entry[3], lambda: map_wait(group, entry).wait_recv())
+                cols_ref[pl.ds(entry[0], 1), :] = near_maps[entry[0]]
+        turned = jnp.transpose(cols_ref[...].astype(F32))
+        targets = lax.broadcasted_iota(jnp.int32, (face, own), 1).astype(F32)
+        for group in groups:
+            for slot, _, _, _, _ in group.faces:
+                inverse_ref[slot] = found(turned[:, slot : slot + 1], targets)
+
+    def send(stage, j, group, values):
         for at, entry in enumerate(group.faces):
-            send_buf[e, entry[0]] = values[:, at * face : (at + 1) * face]
+            send_buf[stage, j, entry[0], height_of(stage)] = (
+                values[:, at * face : (at + 1) * face]
+            )
 
         def start(entry, when=None):
             exists = entry[3]
             if when is not None:
                 exists = when if exists is None else jnp.logical_and(exists, when)
-            guarded(exists, lambda: face_copy(e, group, entry).start())
+            guarded(exists, lambda: face_copy(stage, j, group, entry).start())
 
         if group is final and len(group.faces) == 2:
             odd = lax.rem(here[group.axis], 2) == 1
@@ -293,7 +354,7 @@
             for entry in group.faces:
                 start(entry)
 
-    def precondition(e, ready):
+    def precondition(j, ready):
         pair = split(t_ref[...])
         first = True
         for group in sending:
@@ -301,30 +362,20 @@
             if first:
                 ready()
                 first = False
-            send(e, group, values)
+            send(0, j, group, rounded(0, values))
         base_ref[...] = merge(mm(pair, b_ref[:, own_columns]))
 
     def iteration(j, carry):
-        first, second, third = 3 * j, 3 * j + 1, 3 * j + 2
         start_sums(j)
 
-        @pl.when(j == 0)
-        def _():
-            for group in groups:
-                for at, entry in enumerate(group.faces):
-                    guarded(entry[3], lambda: map_wait(group, entry).wait_recv())
-                    row = near_maps[entry[0]]
-                    hot = lax.broadcasted_iota(jnp.int32, (own, face), 0) == row
-                    hot = jnp.where(hot, 1.0, 0.0)
-                    part = pl.ds(group.packed.start + at * face, face)
-                    gather_ref[:, part] = hot.astype(BF16)
-                    scatter_ref[part, :] = jnp.transpose(hot).astype(BF16)
-
-        prepared = scattered(first, base_ref[...])
-        rounded = prepared.astype(BF16)
+        pl.when(j == 0)(invert)
+
+        prepared = scattered(0, j, base_ref[...])
+        pair = split(prepared)
         for group in sending:
-            send(second, group, mm(rounded, gather_ref[:, group.packed]))
-        pair = split(prepared)
+            taken = [take(prepared, near_maps[entry[0]]) for entry in group.faces]
+            values = taken[0] if len(taken) == 1 else jnp.concatenate(taken, axis=1)
+            send(1, j, group, rounded(1, values))
         pass_sums(j)
 
         @pl.when(j == 0)
@@ -340,16 +391,17 @@
             load_ghosts.wait()
 
         for group in arriving[:-1]:
-            values = arrived(second, group)
+            values = arrived(1, j, group)
             for columns in targets:
-                acc_ref[:, columns] += mm(values, k_ref[group.columns, columns])
-        values = arrived(second, final)
+                acc_ref[:, columns] += joined(1, mm(values, k_ref[group.columns, columns]))
+        values = arrived(1, j, final)
 
         def products(columns):
-            return acc_ref[:, columns] + mm(values, k_ref[final.columns, columns])
+            product = mm(values, k_ref[final.columns, columns])
+            return acc_ref[:, columns] + joined(1, product)
 
         for group in sending:
-            send(third, group, products(group.columns))
+            send(2, j, group, rounded(2, products(group.columns)))
         base = products(own_columns)
         finish_sums(j)
         coeffs, height = heights(j, ITERS - 1)
@@ -362,7 +414,7 @@
         newest = newest * inverse
         v_ref[j] = newest
         last_ref[...] = newest
-        applied = scattered(third, base)
+        applied = scattered(2, j, base)
         for k in range(ITERS - 1):
             applied = applied - coeffs[k] * w_ref[k]
         applied = applied * inverse
@@ -371,18 +423,22 @@
 
         @pl.when(j < ITERS - 1)
         def _():
-            precondition(3 * j + 3, lambda: None)
+            precondition(j + 1, lambda: None)
 
         return carry
 
     def ready():
         load_own.start()
         load_ghosts.start()
-        pl.semaphore_wait(barrier, len(greeted))
-        for group in groups:
-            for entry in group.faces:
-                guarded(entry[3], lambda: map_copy(group, entry).start())
-
+
+    load_maps.wait()
+    pl.semaphore_wait(barrier, expected)
+    for group in groups:
+        for entry in group.faces:
+            guarded(entry[3], lambda: map_copy(group, entry).start())
+
+    load_g.wait()
+    t_ref[...] = g_ref[...]
     load_b.wait()
     precondition(0, ready)
     lax.fori_loop(0, ITERS, iteration, 0)
@@ -421,8 +477,9 @@
         for entry in group.faces:
             def drain():
                 map_copy(group, entry).wait_send()
-                for e in range(3 * ITERS):
-                    face_copy(e, group, entry).wait_send()
+                for stage in range(3):
+                    for j in range(ITERS):
+                        face_copy(stage, j, group, entry).wait_send()
             guarded(entry[3], drain)
     for r in range(ITERS if direct else ITERS + 1):
         for peer in plane:
@@ -441,7 +498,6 @@
     maps = jnp.swapaxes(face_maps[0, 0], 0, 1)
     face = maps.shape[-1]
     whole = local_schur.shape[-1]
-    exchanges = 3 * ITERS
     sums = ITERS + 1
     count = nx * ny * nz
     direct = count if count <= DIRECT_MAX else 1
@@ -451,16 +507,18 @@
     packed = pl.pallas_call(
         functools.partial(kernel, sizes),
         out_shape=pltpu.VMEM((rhs + 8, own), F32),
-        in_specs=[vmem, vmem, hbm, hbm],
+        in_specs=[hbm, hbm, hbm, hbm],
         out_specs=vmem,
         scratch_shapes=[
+            pltpu.VMEM((rhs, own), F32),
+            pltpu.VMEM(maps.shape, jnp.int32),
             pltpu.VMEM((whole, whole), BF16),
             pltpu.VMEM((own, whole), BF16),
             pltpu.VMEM(maps.shape, jnp.int32),
-            pltpu.VMEM((own, 6 * face), BF16),
-            pltpu.VMEM((6 * face, own), BF16),
-            pltpu.VMEM((exchanges, 6, rhs, face), BF16),
-            pltpu.VMEM((exchanges, 6, rhs, face), BF16),
+            pltpu.VMEM((8, face), jnp.int32),
+            pltpu.VMEM((6, 1, own), jnp.int32),
+            pltpu.VMEM((3, ITERS, 6, 2 * rhs, face), BF16),
+            pltpu.VMEM((3, ITERS, 6, 2 * rhs, face), BF16),
             pltpu.VMEM((rhs, whole), F32),
             pltpu.VMEM((rhs, own), F32),
             pltpu.VMEM((rhs, own), F32),
@@ -472,11 +530,11 @@
             pltpu.VMEM((sums, nx * ny, 1, 128), F32),
             pltpu.VMEM((sums, nz, 1, 128), F32),
             pltpu.VMEM((direct, 1, 128), F32),
-            dma((3,)),
+            dma((5,)),
             dma((6,)),
             dma((6,)),
-            dma((exchanges, 6)),
-            dma((exchanges, 6)),
+            dma((3, ITERS, 6)),
+            dma((3, ITERS, 6)),
             dma((sums, nx * ny)),
             dma((sums, nx * ny)),
             dma((sums, nz)),

time: 46.9 us -> 46.4 us (0.989)
  Pallas kernels: 45 us -> 44.5 us
    pallas_call x1, Pallas kernels: 45 us -> 44.5 us  [local(): pl.pallas_call(functools.partial(kernel, sizes), out_shape=pltpu.VMEM((rh...]
where the time goes in v2:
time: 46.4 us; the launch traced here: 46.2 us
  Pallas kernels  44.5 us (96%)
  local copies, waits for them, and re-layouts  1.13 us (2%)
  between operations  0.64 us (1%)
    pallas_call x1, Pallas kernels, local(): pl.pallas_call(functools.partial(kernel, sizes), out_shape=pltpu.VMEM((rh...  44.5 us

profile of v2, /device:TPU:0, one launch (start us, length us, event | category | flops | bytes accessed | tf_op | source)
XLA Modules:
  0.0 46.2 jit_solution(14842072063802757078)
XLA Ops:
  0.6 44.5 %shard_map.59 = f32[24,512]{1,0:T(8,128)S(1)} custom-call(f32[16,512]{1,0:T(8,128)} %bitcast.10, s32[6,1,256]{2,1,0:T(1,128)} %bitcast.11, bf16[2048,2048]{1,0:T(8,128)(2,1)} %bitcast.8, bf16[512,2048]{1,0:T(8,128)(2,1)} %bitcast.9), custom_call_target="tpu_custom_call" | custom-call | tf_op jit(solution)/shard_map/pallas_call | solution.py:507
  45.1 0.5 %slice_bitcast_fusion.1 = f32[16]{0:T(128)} fusion(f32[24,512]{1,0:T(8,128)S(1)} %shard_map.59), kind=kLoop, calls=%fused_computation.1 | loop fusion | bytes 128 | tf_op jit(solution)/shard_map/squeeze | solution.py:549
  45.6 0.6 %slice_bitcast_fusion = f32[1,1,1,16,512]{4,3,2,1,0:T(8,128)} fusion(f32[24,512]{1,0:T(8,128)S(1)} %shard_map.59), kind=kLoop, calls=%fused_computation | loop fusion | bytes 65536 | tf_op jit(solution)/shard_map/broadcast_in_dim | solution.py:549

commit v3 on v2

--- a/solution.py
+++ b/solution.py
@@ -13,7 +13,7 @@
 BF16 = jnp.bfloat16
 F32 = jnp.float32
 DIRECT_MAX = 32
-PAIRED = (False, True, True)
+PAIRED = (False, True, False)
 
 
 def split(x):
@@ -455,7 +455,22 @@
     for section in range(ITERS - 1):
         coeffs, height = heights(section + 1, section + 1)
         rotate_column(coeffs + [height], section, cosines, sines, rhs_vec, triangle)
+    for group in groups:
+        for entry in group.faces:
+            def drain():
+                map_copy(group, entry).wait_send()
+                for stage in range(3):
+                    for j in range(ITERS):
+                        face_copy(stage, j, group, entry).wait_send()
+            guarded(entry[3], drain)
+    for r in range(ITERS if direct else ITERS + 1):
+        for peer in plane:
+            plane_copy(r, peer, ix * ny + iy).wait_send()
+        for peer in line:
+            line_copy(r, peer, iz).wait_send()
     if direct:
+        for peer in others:
+            all_copy(peer, rank(here)).wait_send()
         for peer in others:
             all_copy(peer, rank(peer)).wait_recv()
         total = jnp.sum(all_buf[...], axis=0)
@@ -472,23 +487,6 @@
     ratio = jnp.abs(rhs_vec[ITERS]) / beta_norm
     ratio = jnp.sum(jnp.where(rows == lanes, ratio, 0.0), axis=0, keepdims=True)
     out_ref[pl.ds(rhs, 8), pl.ds(0, 128)] = jnp.broadcast_to(ratio, (8, 128))
-
-    for group in groups:
-        for entry in group.faces:
-            def drain():
-                map_copy(group, entry).wait_send()
-                for stage in range(3):
-                    for j in range(ITERS):
-                        face_copy(stage, j, group, entry).wait_send()
-            guarded(entry[3], drain)
-    for r in range(ITERS if direct else ITERS + 1):
-        for peer in plane:
-            plane_copy(r, peer, ix * ny + iy).wait_send()
-        for peer in line:
-            line_copy(r, peer, iz).wait_send()
-    if direct:
-        for peer in others:
-            all_copy(peer, rank(here)).wait_send()
 
 
 def local(sizes, gradient, local_schur, inverse_rows, face_maps):

time: 46.4 us -> 45.8 us (0.987)
  Pallas kernels: 44.5 us -> 43.8 us
    pallas_call x1, Pallas kernels: 44.5 us -> 43.8 us  [local(): pl.pallas_call(functools.partial(kernel, sizes), out_shape=pltpu.VMEM((rh...]
where the time goes in v3:
time: 45.8 us; the launch traced here: 45.6 us
  Pallas kernels  43.8 us (96%)
  local copies, waits for them, and re-layouts  1.13 us (2%)
  between operations  0.64 us (1%)
    pallas_call x1, Pallas kernels, local(): pl.pallas_call(functools.partial(kernel, sizes), out_shape=pltpu.VMEM((rh...  43.8 us

profile of v3, /device:TPU:0, one launch (start us, length us, event | category | flops | bytes accessed | tf_op | source)
XLA Modules:
  0.0 45.6 jit_solution(1044203565396209728)
XLA Ops:
  0.6 43.8 %shard_map.59 = f32[24,512]{1,0:T(8,128)S(1)} custom-call(f32[16,512]{1,0:T(8,128)} %bitcast.10, s32[6,1,256]{2,1,0:T(1,128)} %bitcast.11, bf16[2048,2048]{1,0:T(8,128)(2,1)} %bitcast.8, bf16[512,2048]{1,0:T(8,128)(2,1)} %bitcast.9), custom_call_target="tpu_custom_call" | custom-call | tf_op jit(solution)/shard_map/pallas_call | solution.py:505
  44.4 0.5 %slice_bitcast_fusion.1 = f32[16]{0:T(128)} fusion(f32[24,512]{1,0:T(8,128)S(1)} %shard_map.59), kind=kLoop, calls=%fused_computation.1 | loop fusion | bytes 128 | tf_op jit(solution)/shard_map/squeeze | solution.py:547
  45.0 0.6 %slice_bitcast_fusion = f32[1,1,1,16,512]{4,3,2,1,0:T(8,128)} fusion(f32[24,512]{1,0:T(8,128)S(1)} %shard_map.59), kind=kLoop, calls=%fused_computation | loop fusion | bytes 65536 | tf_op jit(solution)/shard_map/broadcast_in_dim | solution.py:547

commit v4 on v3

--- a/solution.py
+++ b/solution.py
@@ -382,23 +382,32 @@
         def _():
             load_own.wait()
 
-        targets = [group.columns for group in sending] + [own_columns]
-        for columns in targets:
+        urgent = [group.columns for group in sending if group.axis != 1]
+        patient = [group.columns for group in sending if group.axis == 1] + [own_columns]
+        for columns in urgent + patient:
             acc_ref[:, columns] = merge(mm(pair, k_ref[own_columns, columns]))
 
         @pl.when(j == 0)
         def _():
             load_ghosts.wait()
 
+        late = []
         for group in arriving[:-1]:
             values = arrived(1, j, group)
-            for columns in targets:
+            if group.axis != 1:
+                late.append((group, values))
+            for columns in urgent + (patient if group.axis == 1 else []):
                 acc_ref[:, columns] += joined(1, mm(values, k_ref[group.columns, columns]))
         values = arrived(1, j, final)
 
         def products(columns):
-            product = mm(values, k_ref[final.columns, columns])
-            return acc_ref[:, columns] + joined(1, product)
+            rest = [(final, values)]
+            if not any(columns is other for other in urgent):
+                rest = late + rest
+            total = acc_ref[:, columns]
+            for group, block in rest:
+                total = total + joined(1, mm(block, k_ref[group.columns, columns]))
+            return total
 
         for group in sending:
             send(2, j, group, rounded(2, products(group.columns)))

time: 45.8 us -> 45.3 us (0.989)
  Pallas kernels: 43.8 us -> 43.3 us
where the time goes in v4:
time: 45.3 us; the launch traced here: 45.1 us
  Pallas kernels  43.3 us (96%)
  local copies, waits for them, and re-layouts  1.13 us (2%)
  between operations  0.64 us (1%)
    pallas_call x1, Pallas kernels, local(): pl.pallas_call(functools.partial(kernel, sizes), out_shape=pltpu.VMEM((rh...  43.3 us

profile of v4, /device:TPU:0, one launch (start us, length us, event | category | flops | bytes accessed | tf_op | source)
XLA Modules:
  0.0 45.1 jit_solution(12370991544863356035)
XLA Ops:
  0.6 43.3 %shard_map.59 = f32[24,512]{1,0:T(8,128)S(1)} custom-call(f32[16,512]{1,0:T(8,128)} %bitcast.10, s32[6,1,256]{2,1,0:T(1,128)} %bitcast.11, bf16[2048,2048]{1,0:T(8,128)(2,1)} %bitcast.8, bf16[512,2048]{1,0:T(8,128)(2,1)} %bitcast.9), custom_call_target="tpu_custom_call" | custom-call | tf_op jit(solution)/shard_map/pallas_call | solution.py:514
  44.0 0.5 %slice_bitcast_fusion.1 = f32[16]{0:T(128)} fusion(f32[24,512]{1,0:T(8,128)S(1)} %shard_map.59), kind=kLoop, calls=%fused_computation.1 | loop fusion | bytes 128 | tf_op jit(solution)/shard_map/squeeze | solution.py:556
  44.5 0.6 %slice_bitcast_fusion = f32[1,1,1,16,512]{4,3,2,1,0:T(8,128)} fusion(f32[24,512]{1,0:T(8,128)S(1)} %shard_map.59), kind=kLoop, calls=%fused_computation | loop fusion | bytes 65536 | tf_op jit(solution)/shard_map/broadcast_in_dim | solution.py:556

commit v5 on v4

--- a/solution.py
+++ b/solution.py
@@ -376,7 +376,6 @@
             taken = [take(prepared, near_maps[entry[0]]) for entry in group.faces]
             values = taken[0] if len(taken) == 1 else jnp.concatenate(taken, axis=1)
             send(1, j, group, rounded(1, values))
-        pass_sums(j)
 
         @pl.when(j == 0)
         def _():
@@ -386,6 +385,7 @@
         patient = [group.columns for group in sending if group.axis == 1] + [own_columns]
         for columns in urgent + patient:
             acc_ref[:, columns] = merge(mm(pair, k_ref[own_columns, columns]))
+        pass_sums(j)
 
         @pl.when(j == 0)
         def _():

time: 45.3 us -> 45.3 us (level)
  no operation moved by 1% of the time
where the time goes in v5:
time: 45.3 us; the launch traced here: 45.1 us
  Pallas kernels  43.4 us (96%)
  local copies, waits for them, and re-layouts  1.13 us (2%)
  between operations  0.64 us (1%)
    pallas_call x1, Pallas kernels, local(): pl.pallas_call(functools.partial(kernel, sizes), out_shape=pltpu.VMEM((rh...  43.4 us

profile of v5, /device:TPU:0, one launch (start us, length us, event | category | flops | bytes accessed | tf_op | source)
XLA Modules:
  0.0 45.1 jit_solution(13249022988600195716)
XLA Ops:
  0.6 43.4 %shard_map.59 = f32[24,512]{1,0:T(8,128)S(1)} custom-call(f32[16,512]{1,0:T(8,128)} %bitcast.10, s32[6,1,256]{2,1,0:T(1,128)} %bitcast.11, bf16[2048,2048]{1,0:T(8,128)(2,1)} %bitcast.8, bf16[512,2048]{1,0:T(8,128)(2,1)} %bitcast.9), custom_call_target="tpu_custom_call" | custom-call | tf_op jit(solution)/shard_map/pallas_call | solution.py:514
  44.0 0.5 %slice_bitcast_fusion.1 = f32[16]{0:T(128)} fusion(f32[24,512]{1,0:T(8,128)S(1)} %shard_map.59), kind=kLoop, calls=%fused_computation.1 | loop fusion | bytes 128 | tf_op jit(solution)/shard_map/squeeze | solution.py:556
  44.5 0.6 %slice_bitcast_fusion = f32[1,1,1,16,512]{4,3,2,1,0:T(8,128)} fusion(f32[24,512]{1,0:T(8,128)S(1)} %shard_map.59), kind=kLoop, calls=%fused_computation | loop fusion | bytes 65536 | tf_op jit(solution)/shard_map/broadcast_in_dim | solution.py:556
